TPU v7x, 32 devices: a whole 2x2x4 slice. The times are simulated.
32 devices in a mesh: rep: 2 (over x), fsdp: 16 (over z, y, core).
Axes of the slice: x: 2, y: 2, z: 4, core: 2. Of those that a mesh axis runs over, the one named last changes fastest.
Arguments:
- tokens: bfloat16 [256, 3584], P(('rep', 'fsdp')), may hold values from -6 to 6
- targets: bfloat16 [256, 3584], P(('rep', 'fsdp')), may hold values from -6 to 6
- gate_weight: bfloat16 [3584, 18944], P(None, 'fsdp'), may hold values from -0.09375 to 0.09375
- up_weight: bfloat16 [3584, 18944], P(None, 'fsdp'), may hold values from -0.09375 to 0.09375
- down_weight: bfloat16 [18944, 3584], P('fsdp'), may hold values from -0.046875 to 0.046875
- gate_direction: bfloat16 [3584, 18944], P(None, 'fsdp'), may hold values from -0.09375 to 0.09375
- up_direction: bfloat16 [3584, 18944], P(None, 'fsdp'), may hold values from -0.09375 to 0.09375
- down_direction: bfloat16 [18944, 3584], P('fsdp'), may hold values from -0.046875 to 0.046875
Outputs:
- hvp_gate: float32 [3584, 18944], P(None, 'fsdp')
- hvp_up: float32 [3584, 18944], P(None, 'fsdp')
- hvp_down: float32 [18944, 3584], P('fsdp')
All inputs are finite; a program needn't handle non-finite values.
Results may differ from a plain program's by a relative error of at most 0.0069.
Values may be sent and summed in bfloat16 or wider, within the bound.
A program may use at most 192 MiB of HBM per device.

v0:
```python
import jax
import jax.numpy as jnp
from jax import lax
from jax.sharding import PartitionSpec as P


def silu_parts(gate):
    sigmoid_value = jax.nn.sigmoid(gate)
    slope = sigmoid_value * (1.0 + gate * (1.0 - sigmoid_value))
    bend = sigmoid_value * (1.0 - sigmoid_value) * (2.0 + gate * (1.0 - 2.0 * sigmoid_value))
    return (gate * sigmoid_value, slope, bend)


def inner_rows(left, right):
    return lax.dot_general(
        left, right, (((0,), (0,)), ((), ())), preferred_element_type=jnp.float32
    )


def products(
    gathered,
    gate_grad_tangent,
    up_grad_tangent,
    hidden,
    hidden_tangent,
    error_all,
    error_tangent_all,
):
    hvp_gate = inner_rows(gathered, gate_grad_tangent)
    hvp_up = inner_rows(gathered, up_grad_tangent)
    hvp_down = inner_rows(hidden_tangent, error_all) + inner_rows(hidden, error_tangent_all)
    return (hvp_gate, hvp_up, hvp_down)


def on_device(
    tokens,
    targets,
    gate_weight,
    up_weight,
    down_weight,
    gate_direction,
    up_direction,
    down_direction,
):
    width = tokens.shape[1]
    gathered = lax.all_gather(tokens, "fsdp", axis=0, tiled=True)
    gate = jnp.dot(gathered, gate_weight, preferred_element_type=jnp.float32)
    up = jnp.dot(gathered, up_weight, preferred_element_type=jnp.float32)
    gate_tangent = jnp.dot(gathered, gate_direction, preferred_element_type=jnp.float32)
    up_tangent = jnp.dot(gathered, up_direction, preferred_element_type=jnp.float32)
    activation, slope, bend = silu_parts(gate)
    hidden = (activation * up).astype(jnp.bfloat16)
    hidden_tangent = (slope * gate_tangent * up + activation * up_tangent).astype(jnp.bfloat16)
    primal = jnp.dot(hidden, down_weight, preferred_element_type=jnp.float32)
    tangent = jnp.dot(hidden_tangent, down_weight, preferred_element_type=jnp.float32) + jnp.dot(
        hidden, down_direction, preferred_element_type=jnp.float32
    )
    summed = lax.psum_scatter(
        jnp.concatenate([primal, tangent], axis=1), "fsdp", scatter_dimension=0, tiled=True
    )
    error = (summed[:, :width] - targets.astype(jnp.float32)).astype(jnp.bfloat16)
    error_tangent = summed[:, width:].astype(jnp.bfloat16)
    error_all, error_tangent_all = (
        lax.all_gather(error, "fsdp", axis=0, tiled=True),
        lax.all_gather(error_tangent, "fsdp", axis=0, tiled=True),
    )
    back = jnp.dot(error_all, down_weight.T, preferred_element_type=jnp.float32)
    back_tangent = jnp.dot(
        error_tangent_all, down_weight.T, preferred_element_type=jnp.float32
    ) + jnp.dot(error_all, down_direction.T, preferred_element_type=jnp.float32)
    gate_grad_tangent = (
        back_tangent * up * slope + back * up_tangent * slope + back * up * bend * gate_tangent
    ).astype(jnp.bfloat16)
    up_grad_tangent = (back_tangent * activation + back * slope * gate_tangent).astype(jnp.bfloat16)
    pair_rows = (
        lax.all_gather(gathered, "rep", axis=0, tiled=True),
        lax.all_gather(gate_grad_tangent, "rep", axis=0, tiled=True),
        lax.all_gather(up_grad_tangent, "rep", axis=0, tiled=True),
        lax.all_gather(hidden, "rep", axis=0, tiled=True),
        lax.all_gather(hidden_tangent, "rep", axis=0, tiled=True),
        lax.all_gather(error_all, "rep", axis=0, tiled=True),
        lax.all_gather(error_tangent_all, "rep", axis=0, tiled=True),
    )
    hvp_gate, hvp_up, hvp_down = products(
        pair_rows[0],
        pair_rows[1],
        pair_rows[2],
        pair_rows[3],
        pair_rows[4],
        pair_rows[5],
        pair_rows[6],
    )
    return (hvp_gate, hvp_up, hvp_down)


def solution(mesh):
    in_specs = (
        P(("rep", "fsdp"), None),
        P(("rep", "fsdp"), None),
        P(None, "fsdp"),
        P(None, "fsdp"),
        P("fsdp", None),
        P(None, "fsdp"),
        P(None, "fsdp"),
        P("fsdp", None),
    )
    out_specs = (P(None, "fsdp"), P(None, "fsdp"), P("fsdp", None))
    return jax.shard_map(
        on_device, mesh=mesh, in_specs=in_specs, out_specs=out_specs, check_vma=False
    )
```

profile of v0, /device:TPU:0, one launch (start us, length us, event | category | flops | bytes accessed | tf_op | source)
XLA Modules:
  0.0 296.1 jit_solution(9094616543245920694)
XLA Ops:
  8.0 0.0 reduce-scatter.2.cloned.1.call-start
  8.0 26.1 %all_gather.30 = bf16[128,3584]{1,0:T(8,128)(2,1)S(1)} all-gather(bf16[8,3584]{1,0:T(8,128)(2,1)} %param.8), channel_id=1, replica_groups=mesh['rep'=2,'fsdp'=16] {'fsdp'}, dimensions={0}, use_global_device_ids=true | all-gather | bytes 974848 | tf_op jit(solution)/shard_map/all_gather | solution.py:46
  34.2 6.1 %fusion.12 = f32[128,1184]{0,1:T(8,128)S(1)} fusion(bf16[128,3584]{1,0:T(8,128)(2,1)S(1)} %all_gather.30, bf16[3584,1184]{0,1:T(8,128)(2,1)} %param.14), kind=kOutput, calls=%fused_computation.26 | convolution fusion | flops 1086324736 | bytes 10010624 | tf_op jit(solution)/shard_map/dot_general | solution.py:50
  40.4 0.0 copy-done.1
  40.4 0.0 copy-start.5
  40.4 0.0 slice-start.8
  40.4 0.0 slice-start.9
  40.4 0.0 slice-start.10
  40.4 2.4 fusion.11
  42.8 0.0 slice-done.6
  42.8 0.2 slice-done.7
  43.0 0.1 slice-done.8
  43.0 2.4 fusion.9
  45.4 0.0 copy-done
  45.4 0.0 copy-done.5
  45.4 0.0 copy-done.7
  45.4 0.0 slice-done.9
  45.4 0.4 slice-done.10
  45.8 0.0 slice-done.11
  45.8 3.3 %multiply_convert_fusion = (bf16[128,1184]{0,1:T(8,128)(2,1)S(1)}, bf16[128,1184]{0,1:T(8,128)(2,1)S(1)}, f32[128,1184]{0,1:T(8,128)}) fusion(f32[128,1184]{0,1:T(8,128)S(1)} %fusion.9, f32[128,1184]{0,1:T(8,128)S(1)} %fusion.12, f32[128,1184]{0,1:T(8,128)S(1)} %fusion.11, bf16[128,3584]{1,0:T(8,128)(2,1)S(1)} %all_gather.30, ...), kind=kOutput, calls=%fused_computation.17 | convolution fusion | flops 1088598016 | bytes 12435456 | tf_op jit(solution)/shard_map/dot_general | solution.py:48
  49.1 0.0 copy-done.9
  49.1 0.0 slice-done
  49.1 0.0 slice-done.1
  49.1 0.0 slice-done.2
  49.1 0.0 slice-start.3
  49.1 0.0 slice-start.4
  49.1 1.4 fusion.13
  50.5 0.0 slice-start.5
  50.5 1.4 fusion.10
  51.9 0.0 slice-done.3
  51.9 0.7 slice-done.4
  52.6 0.1 slice-done.5
  52.6 1.4 convolution_add_fusion.1
  54.0 0.0 copy-start.12
  54.0 2.1 pad_maximum_fusion
  56.1 0.0 reduce-scatter.2.cloned.1.call-update
  56.1 0.0 all-gather.4.cloned.1.call-start
  56.2 0.5 all-gather.4.cloned.1.call-update
  56.7 0.0 all-gather.6.cloned.1.call-start
  56.8 65.3 %reduce-scatter.2.cloned.1.call-done = f32[8,7168]{1,0:T(8,128)} async-done(((f32[128,7168]{1,0:T(8,128)}), f32[8,7168]{1,0:T(8,128)}) %reduce-scatter.2.cloned.1.call-update) | async-done | bytes 229392 | tf_op jit(solution)/shard_map/reduce_scatter | solution.py:58
  122.1 0.0 copy-done.12
  122.1 0.9 fusion.8
  123.0 23.4 %all_gather.32 = bf16[128,3584]{1,0:T(8,128)(2,1)} all-gather(bf16[8,3584]{1,0:T(8,128)(2,1)S(1)} %fusion.8), channel_id=1, replica_groups=mesh['rep'=2,'fsdp'=16] {'fsdp'}, dimensions={0}, use_global_device_ids=true | all-gather | bytes 974848 | tf_op jit(solution)/shard_map/all_gather | solution.py:64
  146.4 0.0 all-gather.6.cloned.1.call-update
  146.4 0.0 all-gather.8.cloned.1.call-start
  146.4 13.5 %all_gather.36 = bf16[256,1184]{0,1:T(8,128)(2,1)S(1)} all-gather(bf16[128,1184]{0,1:T(8,128)(2,1)S(1)} %get-tuple-element.6), channel_id=1, replica_groups=mesh['rep'=2,'fsdp'=16] {'rep'}, dimensions={0}, use_global_device_ids=true | all-gather | bytes 909312 | tf_op jit(solution)/shard_map/all_gather | solution.py:80
  159.9 17.0 %all_gather.38 = bf16[256,1184]{0,1:T(8,128)(2,1)S(1)} all-gather(bf16[128,1184]{0,1:T(8,128)(2,1)S(1)} %get-tuple-element.5), channel_id=1, replica_groups=mesh['rep'=2,'fsdp'=16] {'rep'}, dimensions={0}, use_global_device_ids=true | all-gather | bytes 909312 | tf_op jit(solution)/shard_map/all_gather | solution.py:79
  176.9 0.9 slice.15
  177.8 20.2 %all_gather.31 = bf16[128,3584]{1,0:T(8,128)(2,1)S(1)} all-gather(bf16[8,3584]{1,0:T(8,128)(2,1)S(1)} %slice.15), channel_id=1, replica_groups=mesh['rep'=2,'fsdp'=16] {'fsdp'}, dimensions={0}, use_global_device_ids=true | all-gather | bytes 974848 | tf_op jit(solution)/shard_map/all_gather | solution.py:65
  198.1 7.0 %fusion.14 = f32[128,1184]{0,1:T(8,128)} fusion(bf16[128,3584]{1,0:T(8,128)(2,1)S(1)} %all_gather.31, bf16[1184,3584]{1,0:T(8,128)(2,1)} %param.12), kind=kOutput, calls=%fused_computation.28 | convolution fusion | flops 1086324736 | bytes 10010624 | tf_op jit(solution)/shard_map/dot_general | solution.py:68
  205.0 0.0 copy-done.2
  205.0 0.0 all-gather.8.cloned.1.call-update
  205.0 0.0 copy-done.3
  205.1 0.0 copy-start.8
  205.1 0.0 copy-start.10
  205.1 0.0 copy-start.11
  205.1 6.0 %convolution_add_fusion.2 = f32[128,1184]{0,1:T(8,128)S(1)} fusion(f32[128,1184]{0,1:T(8,128)} %fusion.14, bf16[128,3584]{1,0:T(8,128)(2,1)S(1)} %copy-done.3, bf16[1184,3584]{1,0:T(8,128)(2,1)} %param.15), kind=kOutput, calls=%fused_computation.5 | convolution fusion | flops 1086476288 | bytes 10616832 | tf_op jit(solution)/shard_map/dot_general | solution.py:70
  211.2 6.4 %add_convert_fusion = (bf16[128,1184]{0,1:T(8,128)(2,1)S(1)}, bf16[128,1184]{0,1:T(8,128)(2,1)S(1)}) fusion(f32[128,1184]{0,1:T(8,128)S(1)} %copy-done.8, f32[128,1184]{0,1:T(8,128)S(1)} %convolution_add_fusion.2, f32[128,1184]{0,1:T(8,128)S(1)} %copy-done.10, f32[128,1184]{0,1:T(8,128)S(1)} %copy-done.11, f32[128,1184]{0,1:T(8,128)S(1)} %copy-done.6, ...), kind=kOutput, calls=%fused_computation.15 | convolution fusion | flops 1090568192 | bytes 13041664 | tf_op jit(solution)/shard_map/dot_general | solution.py:67
  217.6 17.2 %all_gather.33 = bf16[256,1184]{0,1:T(8,128)(2,1)S(1)} all-gather(bf16[128,1184]{0,1:T(8,128)(2,1)S(1)} %get-tuple-element.4), channel_id=1, replica_groups=mesh['rep'=2,'fsdp'=16] {'rep'}, dimensions={0}, use_global_device_ids=true | all-gather | bytes 909312 | tf_op jit(solution)/shard_map/all_gather | solution.py:77
  234.7 10.2 %convolution_bitcast_fusion.1 = f32[3584,1184]{0,1:T(8,128)} fusion(bf16[256,1184]{0,1:T(8,128)(2,1)S(1)} %all_gather.33, bf16[256,3584]{1,0:T(8,128)(2,1)} %all-gather.4.cloned.1.call-done), kind=kOutput, calls=%fused_computation.2 | convolution fusion | flops 2172649472 | bytes 19415040 | tf_op jit(solution)/shard_map/dot_general | solution.py:15
  245.0 9.9 %all_gather.35 = bf16[256,1184]{0,1:T(8,128)(2,1)S(1)} all-gather(bf16[128,1184]{0,1:T(8,128)(2,1)S(1)} %get-tuple-element.3), channel_id=1, replica_groups=mesh['rep'=2,'fsdp'=16] {'rep'}, dimensions={0}, use_global_device_ids=true | all-gather | bytes 909312 | tf_op jit(solution)/shard_map/all_gather | solution.py:78
  254.9 8.6 %convolution_bitcast_fusion = f32[3584,1184]{0,1:T(8,128)} fusion(bf16[256,1184]{0,1:T(8,128)(2,1)S(1)} %all_gather.35, bf16[256,3584]{1,0:T(8,128)(2,1)S(1)} %copy-done.4), kind=kOutput, calls=%fused_computation.1 | convolution fusion | flops 2172649472 | bytes 19415040 | tf_op jit(solution)/shard_map/dot_general | solution.py:15
  263.5 10.1 %fusion.15 = f32[1184,3584]{1,0:T(8,128)} fusion(bf16[256,1184]{0,1:T(8,128)(2,1)S(1)} %all_gather.36, bf16[256,3584]{1,0:T(8,128)(2,1)} %all-gather.6.cloned.1.call-done), kind=kOutput, calls=%fused_computation.29 | convolution fusion | flops 2172649472 | bytes 19415040 | tf_op jit(solution)/shard_map/dot_general | solution.py:15
  273.6 15.0 %convolution_add_fusion = f32[1184,3584]{1,0:T(8,128)} fusion(f32[1184,3584]{1,0:T(8,128)} %fusion.15, bf16[256,1184]{0,1:T(8,128)(2,1)S(1)} %all_gather.38, bf16[256,3584]{1,0:T(8,128)(2,1)} %all-gather.8.cloned.1.call-done), kind=kOutput, calls=%fused_computation | convolution fusion | flops 2176892928 | bytes 36388864 | tf_op jit(solution)/shard_map/dot_general | solution.py:15
  (26 shorter events, 0.0 us)
Async XLA Ops:
  8.0 114.1 %reduce-scatter.2.cloned.1.call-start = ((), (), s32[]{:S(2)}) async-start(), calls=%async_computation.1 | async-start | bytes 3899392 | tf_op jit(solution)/shard_map/reduce_scatter | solution.py:58
  34.2 11.2 %copy-start = (bf16[128,3584]{1,0:T(8,128)(2,1)}, bf16[128,3584]{1,0:T(8,128)(2,1)S(1)}, u32[]{:S(2)}) copy-start(bf16[128,3584]{1,0:T(8,128)(2,1)S(1)} %all_gather.30) | copy-start | bytes 2752516
  34.2 6.2 %copy-start.1 = (bf16[3584,1184]{0,1:T(8,128)(2,1)S(1)}, bf16[3584,1184]{0,1:T(8,128)(2,1)}, u32[]{:S(2)}) copy-start(bf16[3584,1184]{0,1:T(8,128)(2,1)} %param.13) | copy-start | bytes 25460740
  34.2 8.6 %slice-start.6 = ((s8[8486912]{0:T(1024)(128)(4,1)}), s8[4194304]{0:T(1024)(128)(4,1)S(1)}, s32[]{:S(2)}) async-start(s8[8486912]{0:T(1024)(128)(4,1)} %bitcast.36), calls=%async_computation.11 | async-start | bytes 8388608
  34.2 8.8 %slice-start.7 = ((s8[8486912]{0:T(1024)(128)(4,1)}), s8[4194304]{0:T(1024)(128)(4,1)S(1)}, s32[]{:S(2)}) async-start(s8[8486912]{0:T(1024)(128)(4,1)} %bitcast.36), calls=%async_computation.12 | async-start | bytes 8388608
  40.4 5.0 %copy-start.5 = (f32[128,1184]{0,1:T(8,128)}, f32[128,1184]{0,1:T(8,128)S(1)}, u32[]{:S(2)}) copy-start(f32[128,1184]{0,1:T(8,128)S(1)} %fusion.12) | copy-start | bytes 1818628
  40.4 2.6 slice-start.8
  40.4 5.0 %slice-start.9 = ((s8[8486912]{0:T(1024)(128)(4,1)}), s8[4194304]{0:T(1024)(128)(4,1)S(1)}, s32[]{:S(2)}) async-start(s8[8486912]{0:T(1024)(128)(4,1)} %bitcast.38), calls=%async_computation.14 | async-start | bytes 8388608
  40.4 5.4 %slice-start.10 = ((s8[8486912]{0:T(1024)(128)(4,1)}), s8[4194304]{0:T(1024)(128)(4,1)S(1)}, s32[]{:S(2)}) async-start(s8[8486912]{0:T(1024)(128)(4,1)} %bitcast.38), calls=%async_computation.15 | async-start | bytes 8388608
  43.0 2.4 copy-start.7
  43.0 2.8 slice-start.11
  43.0 6.0 %slice-start = ((s8[8486912]{0:T(1024)(128)(4,1)}), s8[4194304]{0:T(1024)(128)(4,1)S(1)}, s32[]{:S(2)}) async-start(s8[8486912]{0:T(1024)(128)(4,1)} %bitcast.32), calls=%async_computation.5 | async-start | bytes 8388608
  43.0 6.0 %slice-start.1 = ((s8[8486912]{0:T(1024)(128)(4,1)}), s8[4194304]{0:T(1024)(128)(4,1)S(1)}, s32[]{:S(2)}) async-start(s8[8486912]{0:T(1024)(128)(4,1)} %bitcast.32), calls=%async_computation.6 | async-start | bytes 8388608
  45.8 3.3 %copy-start.9 = (f32[128,1184]{0,1:T(8,128)}, f32[128,1184]{0,1:T(8,128)S(1)}, u32[]{:S(2)}) copy-start(f32[128,1184]{0,1:T(8,128)S(1)} %fusion.9) | copy-start | bytes 1818628
  45.8 3.3 %slice-start.2 = ((s8[8486912]{0:T(1024)(128)(4,1)}), s8[98304]{0:T(1024)(128)(4,1)S(1)}, s32[]{:S(2)}) async-start(s8[8486912]{0:T(1024)(128)(4,1)} %bitcast.32), calls=%async_computation.7 | async-start | bytes 196608
  49.1 2.8 slice-start.3
  49.1 3.5 %slice-start.4 = ((s8[8486912]{0:T(1024)(128)(4,1)}), s8[4194304]{0:T(1024)(128)(4,1)S(1)}, s32[]{:S(2)}) async-start(s8[8486912]{0:T(1024)(128)(4,1)} %bitcast.34), calls=%async_computation.9 | async-start | bytes 8388608
  50.5 2.1 slice-start.5
  54.0 68.1 %copy-start.12 = (bf16[8,3584]{1,0:T(8,128)(2,1)S(1)}, bf16[8,3584]{1,0:T(8,128)(2,1)}, u32[]{:S(2)}) copy-start(bf16[8,3584]{1,0:T(8,128)(2,1)} %param.9) | copy-start | bytes 172036
  56.1 178.6 %all-gather.4.cloned.1.call-start = ((), (), s32[]{:S(2)}) async-start(), calls=%async_computation.2 | async-start | bytes 2752512 | tf_op jit(solution)/shard_map/all_gather | solution.py:76
  56.7 206.7 %all-gather.6.cloned.1.call-start = ((), (), s32[]{:S(2)}) async-start(), calls=%async_computation.3 | async-start | bytes 2752512 | tf_op jit(solution)/shard_map/all_gather | solution.py:81
  146.4 127.2 %all-gather.8.cloned.1.call-start = ((), (), s32[]{:S(2)}) async-start(), calls=%async_computation.4 | async-start | bytes 2752512 | tf_op jit(solution)/shard_map/all_gather | solution.py:82
  198.1 7.0 %copy-start.2 = (bf16[128,3584]{1,0:T(8,128)(2,1)}, bf16[128,3584]{1,0:T(8,128)(2,1)S(1)}, u32[]{:S(2)}) copy-start(bf16[128,3584]{1,0:T(8,128)(2,1)S(1)} %all_gather.31) | copy-start | bytes 2752516
  198.1 7.0 %copy-start.3 = (bf16[128,3584]{1,0:T(8,128)(2,1)S(1)}, bf16[128,3584]{1,0:T(8,128)(2,1)}, u32[]{:S(2)}) copy-start(bf16[128,3584]{1,0:T(8,128)(2,1)} %all_gather.32) | copy-start | bytes 2752516
  205.1 6.1 %copy-start.6 = (f32[128,1184]{0,1:T(8,128)S(1)}, f32[128,1184]{0,1:T(8,128)}, u32[]{:S(2)}) copy-start(f32[128,1184]{0,1:T(8,128)} %copy-done.5) | copy-start | bytes 1818628
  205.1 6.1 %copy-start.8 = (f32[128,1184]{0,1:T(8,128)S(1)}, f32[128,1184]{0,1:T(8,128)}, u32[]{:S(2)}) copy-start(f32[128,1184]{0,1:T(8,128)} %copy-done.7) | copy-start | bytes 1818628
  205.1 6.1 %copy-start.10 = (f32[128,1184]{0,1:T(8,128)S(1)}, f32[128,1184]{0,1:T(8,128)}, u32[]{:S(2)}) copy-start(f32[128,1184]{0,1:T(8,128)} %copy-done.9) | copy-start | bytes 1818628
  205.1 6.1 %copy-start.11 = (f32[128,1184]{0,1:T(8,128)S(1)}, f32[128,1184]{0,1:T(8,128)}, u32[]{:S(2)}) copy-start(f32[128,1184]{0,1:T(8,128)} %get-tuple-element.7) | copy-start | bytes 1818628
  234.7 20.1 %copy-start.4 = (bf16[256,3584]{1,0:T(8,128)(2,1)S(1)}, bf16[256,3584]{1,0:T(8,128)(2,1)}, u32[]{:S(2)}) copy-start(bf16[256,3584]{1,0:T(8,128)(2,1)} %all-gather.4.cloned.1.call-done) | copy-start | bytes 5505028
Sparse Core Ops, SparseCore 0:
  56.3 65.7 reduce-scatter.1
Sparse Core Ops, SparseCore 1:
  58.7 27.2 all-gather.3
  146.5 36.4 all-gather.5
  205.1 35.3 all-gather.7
where the time goes:
time: 296 us
  blocking collectives  127 us (43%)
  matrix products  81.6 us (28%)
  waiting for transfers between devices  65.9 us (22%)
  between operations  15.9 us (5%)
  other arithmetic  3 us (1%)
    reduce_scatter x1, waiting for transfers between devices, on_device(): lax.psum_scatter(jnp.concatenate([primal, tangent], axis=1), 'fsdp', scat...  65.3 us
    dot_general x4, matrix products, inner_rows(): lax.dot_general(left, right, (((0,), (0,)), ((), ())), preferred_element_...  43.9 us
    all_gather x1, blocking collectives, on_device(): gathered = lax.all_gather(tokens, 'fsdp', axis=0, tiled=True)  26.1 us
    all_gather x1, blocking collectives, on_device(): lax.all_gather(error, 'fsdp', axis=0, tiled=True)  23.4 us
    all_gather x1, blocking collectives, on_device(): lax.all_gather(error_tangent, 'fsdp', axis=0, tiled=True)  20.2 us
    all_gather x1, blocking collectives, on_device(): lax.all_gather(gate_grad_tangent, 'rep', axis=0, tiled=True)  17.2 us
    all_gather x1, blocking collectives, on_device(): lax.all_gather(hidden, 'rep', axis=0, tiled=True)  17 us
    all_gather x1, blocking collectives, on_device(): lax.all_gather(hidden_tangent, 'rep', axis=0, tiled=True)  13.5 us
  transfers between devices with their start and end apart: 4, of which 1 were waited for; matrix products, arithmetic and copies ran while one was open for 17% of the time, Pallas kernels for 0%

commit v1 on v0

--- a/solution.py
+++ b/solution.py
@@ -62,7 +62,9 @@
     error_tangent = summed[:, width:].astype(jnp.bfloat16)
     error_all, error_tangent_all = (
         lax.all_gather(error, "fsdp", axis=0, tiled=True),
-        lax.all_gather(error_tangent, "fsdp", axis=0, tiled=True),
+        jnp.concatenate(
+            lax.all_to_all(jnp.stack([error_tangent] * lax.axis_size("fsdp")), "fsdp", 0, 0), axis=0
+        ),
     )
     back = jnp.dot(error_all, down_weight.T, preferred_element_type=jnp.float32)
     back_tangent = jnp.dot(

time: 296 us -> 275 us (0.929)
  blocking collectives: 127 us -> 105 us
  matrix products: 81.6 us -> 77.2 us
  starting transfers between devices: 0.17 us -> 4 us
    all_gather x1 -> x0, blocking collectives: 20.2 us -> none  [on_device(): lax.all_gather(error_tangent, 'fsdp', axis=0, tiled=True)]
    all_gather x1, blocking collectives: 17 us -> 9.3 us  [on_device(): lax.all_gather(hidden, 'rep', axis=0, tiled=True)]
    all_gather x1, blocking collectives: 9.9 us -> 17 us  [on_device(): lax.all_gather(up_grad_tangent, 'rep', axis=0, tiled=True)]
    dot_general x1, matrix products: 6.41 us -> 2.64 us  [on_device(): back = jnp.dot(error_all, down_weight.T, preferred_element_type=jnp.float32)]
    all_to_all x0 -> x1, starting transfers between devices: none -> 3.65 us  [on_device(): lax.all_to_all(jnp.stack([error_tangent] * lax.axis_size('fsdp')), 'fsdp'...]
    all_gather x1, blocking collectives: 13.5 us -> 10.2 us  [on_device(): lax.all_gather(hidden_tangent, 'rep', axis=0, tiled=True)]
  transfers between devices with their start and end apart: 4 -> 5, of which waited for: 1 -> 1; matrix products, arithmetic and copies ran while one was open for 17% -> 17% of each run, Pallas kernels for 0% -> 0%
where the time goes in v1:
time: 275 us; the launch traced here: 274 us
  blocking collectives  105 us (38%)
  matrix products  77.2 us (28%)
  waiting for transfers between devices  66 us (24%)
  between operations  16 us (6%)
  starting transfers between devices  4 us (1%)
  local copies, waits for them, and re-layouts  3.33 us (1%)
  other arithmetic  3 us (1%)
    reduce_scatter x1, waiting for transfers between devices, on_device(): lax.psum_scatter(jnp.concatenate([primal, tangent], axis=1), 'fsdp', scat...  65.4 us
    dot_general x4, matrix products, inner_rows(): lax.dot_general(left, right, (((0,), (0,)), ((), ())), preferred_element_...  43.9 us
    all_gather x1, blocking collectives, on_device(): gathered = lax.all_gather(tokens, 'fsdp', axis=0, tiled=True)  26.1 us
    all_gather x1, blocking collectives, on_device(): lax.all_gather(error, 'fsdp', axis=0, tiled=True)  25.2 us
    all_gather x1, blocking collectives, on_device(): lax.all_gather(gate_grad_tangent, 'rep', axis=0, tiled=True)  17.1 us
    all_gather x1, blocking collectives, on_device(): lax.all_gather(up_grad_tangent, 'rep', axis=0, tiled=True)  17 us
    all_gather x1, blocking collectives, on_device(): lax.all_gather(hidden_tangent, 'rep', axis=0, tiled=True)  10.2 us
    all_gather x1, blocking collectives, on_device(): lax.all_gather(hidden, 'rep', axis=0, tiled=True)  9.3 us
  transfers between devices with their start and end apart: 5, of which 1 were waited for; matrix products, arithmetic and copies ran while one was open for 17% of the time, Pallas kernels for 0%

profile of v1, /device:TPU:0, one launch (start us, length us, event | category | flops | bytes accessed | tf_op | source)
XLA Modules:
  0.0 274.3 jit_solution(199361508943241982)
XLA Ops:
  8.0 0.0 reduce-scatter.2.cloned.1.call-start
  8.0 26.1 %all_gather.27 = bf16[128,3584]{1,0:T(8,128)(2,1)S(1)} all-gather(bf16[8,3584]{1,0:T(8,128)(2,1)} %param.8), channel_id=1, replica_groups=mesh['rep'=2,'fsdp'=16] {'fsdp'}, dimensions={0}, use_global_device_ids=true | all-gather | bytes 974848 | tf_op jit(solution)/shard_map/all_gather | solution.py:46
  34.2 6.1 %fusion.14 = f32[128,1184]{0,1:T(8,128)S(1)} fusion(bf16[128,3584]{1,0:T(8,128)(2,1)S(1)} %all_gather.27, bf16[3584,1184]{0,1:T(8,128)(2,1)} %param.14), kind=kOutput, calls=%fused_computation.28 | convolution fusion | flops 1086324736 | bytes 10010624 | tf_op jit(solution)/shard_map/dot_general | solution.py:50
  40.4 0.0 slice-start.11
  40.4 0.0 slice-start.12
  40.4 0.0 slice-start.13
  40.4 2.4 fusion.13
  42.8 0.0 slice-done.9
  42.8 0.2 slice-done.10
  43.0 0.1 slice-done.11
  43.0 2.4 fusion.11
  45.4 0.4 slice-done.13
  45.8 3.2 %multiply_convert_fusion = (bf16[128,1184]{0,1:T(8,128)(2,1)S(1)}, bf16[128,1184]{0,1:T(8,128)(2,1)S(1)}, f32[128,1184]{0,1:T(8,128)}) fusion(f32[128,1184]{0,1:T(8,128)S(1)} %fusion.11, f32[128,1184]{0,1:T(8,128)S(1)} %fusion.14, f32[128,1184]{0,1:T(8,128)S(1)} %fusion.13, bf16[128,3584]{1,0:T(8,128)(2,1)S(1)} %all_gather.27, ...), kind=kOutput, calls=%fused_computation.17 | convolution fusion | flops 1088598016 | bytes 12435456 | tf_op jit(solution)/shard_map/dot_general | solution.py:48
  49.0 0.0 slice-done.2
  49.0 0.0 slice-start.6
  49.1 0.0 slice-start.7
  49.1 1.4 fusion.15
  50.5 0.0 slice-start.8
  50.5 1.4 fusion.12
  51.9 0.7 slice-done.7
  52.5 0.1 slice-done.8
  52.6 1.4 convolution_add_fusion.1
  54.0 0.0 copy-start.12
  54.0 2.1 pad_maximum_fusion
  56.1 0.0 reduce-scatter.2.cloned.1.call-update
  56.1 0.0 all-gather.4.cloned.1.call-start
  56.2 0.5 all-gather.4.cloned.1.call-update
  56.7 65.4 %reduce-scatter.2.cloned.1.call-done = f32[8,7168]{1,0:T(8,128)} async-done(((f32[128,7168]{1,0:T(8,128)}), f32[8,7168]{1,0:T(8,128)}) %reduce-scatter.2.cloned.1.call-update) | async-done | bytes 229392 | tf_op jit(solution)/shard_map/reduce_scatter | solution.py:58
  122.0 0.9 slice.15
  122.9 1.0 stack.2
  123.9 3.6 %all-to-all-start = ((bf16[16,8,3584]{2,1,0:T(8,128)(2,1)}), bf16[16,8,3584]{2,1,0:T(8,128)(2,1)S(1)}, u32[]{:S(2)}, u32[]{:S(2)}) async-start(bf16[16,8,3584]{2,1,0:T(8,128)(2,1)} %stack.2), calls=%async_computation.1 | async-start | bytes 1835008 | tf_op jit(solution)/shard_map/all_to_all | solution.py:66
  127.6 0.0 all-gather.6.cloned.1.call-start
  127.6 10.2 %all_gather.32 = bf16[256,1184]{0,1:T(8,128)(2,1)S(1)} all-gather(bf16[128,1184]{0,1:T(8,128)(2,1)S(1)} %get-tuple-element.6), channel_id=1, replica_groups=mesh['rep'=2,'fsdp'=16] {'rep'}, dimensions={0}, use_global_device_ids=true | all-gather | bytes 909312 | tf_op jit(solution)/shard_map/all_gather | solution.py:82
  137.8 9.3 %all_gather.34 = bf16[256,1184]{0,1:T(8,128)(2,1)S(1)} all-gather(bf16[128,1184]{0,1:T(8,128)(2,1)S(1)} %get-tuple-element.5), channel_id=1, replica_groups=mesh['rep'=2,'fsdp'=16] {'rep'}, dimensions={0}, use_global_device_ids=true | all-gather | bytes 909312 | tf_op jit(solution)/shard_map/all_gather | solution.py:81
  147.1 0.9 fusion.8
  148.0 25.2 %all_gather.28 = bf16[128,3584]{1,0:T(8,128)(2,1)} all-gather(bf16[8,3584]{1,0:T(8,128)(2,1)S(1)} %fusion.8), channel_id=1, replica_groups=mesh['rep'=2,'fsdp'=16] {'fsdp'}, dimensions={0}, use_global_device_ids=true | all-gather | bytes 974848 | tf_op jit(solution)/shard_map/all_gather | solution.py:64
  173.2 0.0 all-gather.6.cloned.1.call-update
  173.2 0.2 all-gather.8.cloned.1.call-start
  173.4 0.0 all-to-all-done
  173.5 0.0 slice-start.3
  173.5 0.0 slice-start.4
  173.5 6.4 %fusion.9 = f32[128,1184]{0,1:T(8,128)S(1)} fusion(bf16[1184,3584]{1,0:T(8,128)(2,1)} %param.12, bf16[16,8,3584]{2,1,0:T(8,128)(2,1)S(1)} %all-to-all-done), kind=kOutput, calls=%fused_computation.23 | convolution fusion | flops 1086324736 | bytes 10010624 | tf_op jit(solution)/shard_map/dot_general | solution.py:70
  179.9 0.0 slice-start.5
  179.9 0.0 copy-start.8
  180.0 0.0 copy-start.10
  180.0 0.0 copy-start.11
  180.0 5.9 %convolution_add_fusion.2 = f32[128,1184]{0,1:T(8,128)S(1)} fusion(f32[128,1184]{0,1:T(8,128)S(1)} %fusion.9, bf16[128,3584]{1,0:T(8,128)(2,1)S(1)} %copy-done.3, bf16[1184,3584]{1,0:T(8,128)(2,1)} %param.15), kind=kOutput, calls=%fused_computation.5 | convolution fusion | flops 1086476288 | bytes 10616832 | tf_op jit(solution)/shard_map/dot_general | solution.py:72
  185.9 0.0 slice-done.3
  185.9 0.0 slice-done.4
  185.9 0.0 slice-done.5
  185.9 0.0 copy-done.6
  186.0 0.0 copy-done.8
  186.0 0.0 copy-done.10
  186.0 0.0 copy-done.11
  186.0 2.6 add_convert_fusion
  188.6 17.1 %all_gather.29 = bf16[256,1184]{0,1:T(8,128)(2,1)S(1)} all-gather(bf16[128,1184]{0,1:T(8,128)(2,1)S(1)} %get-tuple-element.4), channel_id=1, replica_groups=mesh['rep'=2,'fsdp'=16] {'rep'}, dimensions={0}, use_global_device_ids=true | all-gather | bytes 909312 | tf_op jit(solution)/shard_map/all_gather | solution.py:79
  205.7 0.0 all-gather.8.cloned.1.call-update
  205.7 0.0 all-gather.4.cloned.1.call-done
  205.8 0.0 copy-start.4
  205.8 10.3 %convolution_bitcast_fusion.1 = f32[3584,1184]{0,1:T(8,128)} fusion(bf16[256,1184]{0,1:T(8,128)(2,1)S(1)} %all_gather.29, bf16[256,3584]{1,0:T(8,128)(2,1)} %all-gather.4.cloned.1.call-done), kind=kOutput, calls=%fused_computation.2 | convolution fusion | flops 2172649472 | bytes 19415040 | tf_op jit(solution)/shard_map/dot_general | solution.py:15
  216.0 17.0 %all_gather.31 = bf16[256,1184]{0,1:T(8,128)(2,1)S(1)} all-gather(bf16[128,1184]{0,1:T(8,128)(2,1)S(1)} %get-tuple-element.3), channel_id=1, replica_groups=mesh['rep'=2,'fsdp'=16] {'rep'}, dimensions={0}, use_global_device_ids=true | all-gather | bytes 909312 | tf_op jit(solution)/shard_map/all_gather | solution.py:80
  233.0 8.6 %convolution_bitcast_fusion = f32[3584,1184]{0,1:T(8,128)} fusion(bf16[256,1184]{0,1:T(8,128)(2,1)S(1)} %all_gather.31, bf16[256,3584]{1,0:T(8,128)(2,1)S(1)} %copy-done.4), kind=kOutput, calls=%fused_computation.1 | convolution fusion | flops 2172649472 | bytes 19415040 | tf_op jit(solution)/shard_map/dot_general | solution.py:15
  241.6 10.1 %fusion.16 = f32[1184,3584]{1,0:T(8,128)} fusion(bf16[256,1184]{0,1:T(8,128)(2,1)S(1)} %all_gather.32, bf16[256,3584]{1,0:T(8,128)(2,1)} %all-gather.6.cloned.1.call-done), kind=kOutput, calls=%fused_computation.30 | convolution fusion | flops 2172649472 | bytes 19415040 | tf_op jit(solution)/shard_map/dot_general | solution.py:15
  251.7 15.0 %convolution_add_fusion = f32[1184,3584]{1,0:T(8,128)} fusion(f32[1184,3584]{1,0:T(8,128)} %fusion.16, bf16[256,1184]{0,1:T(8,128)(2,1)S(1)} %all_gather.34, bf16[256,3584]{1,0:T(8,128)(2,1)} %all-gather.8.cloned.1.call-done), kind=kOutput, calls=%fused_computation | convolution fusion | flops 2176892928 | bytes 36388864 | tf_op jit(solution)/shard_map/dot_general | solution.py:15
  (35 shorter events, 0.1 us)
Async XLA Ops:
  8.0 114.0 %reduce-scatter.2.cloned.1.call-start = ((), (), s32[]{:S(2)}) async-start(), calls=%async_computation.2 | async-start | bytes 3899392 | tf_op jit(solution)/shard_map/reduce_scatter | solution.py:58
  34.2 11.2 %copy-start = (bf16[128,3584]{1,0:T(8,128)(2,1)}, bf16[128,3584]{1,0:T(8,128)(2,1)S(1)}, u32[]{:S(2)}) copy-start(bf16[128,3584]{1,0:T(8,128)(2,1)S(1)} %all_gather.27) | copy-start | bytes 2752516
  34.2 6.2 %copy-start.1 = (bf16[3584,1184]{0,1:T(8,128)(2,1)S(1)}, bf16[3584,1184]{0,1:T(8,128)(2,1)}, u32[]{:S(2)}) copy-start(bf16[3584,1184]{0,1:T(8,128)(2,1)} %param.13) | copy-start | bytes 25460740
  34.2 8.6 %slice-start.9 = ((s8[8486912]{0:T(1024)(128)(4,1)}), s8[4194304]{0:T(1024)(128)(4,1)S(1)}, s32[]{:S(2)}) async-start(s8[8486912]{0:T(1024)(128)(4,1)} %bitcast.40), calls=%async_computation.15 | async-start | bytes 8388608
  34.2 8.8 %slice-start.10 = ((s8[8486912]{0:T(1024)(128)(4,1)}), s8[4194304]{0:T(1024)(128)(4,1)S(1)}, s32[]{:S(2)}) async-start(s8[8486912]{0:T(1024)(128)(4,1)} %bitcast.40), calls=%async_computation.16 | async-start | bytes 8388608
  40.4 5.0 %copy-start.5 = (f32[128,1184]{0,1:T(8,128)}, f32[128,1184]{0,1:T(8,128)S(1)}, u32[]{:S(2)}) copy-start(f32[128,1184]{0,1:T(8,128)S(1)} %fusion.14) | copy-start | bytes 1818628
  40.4 2.6 slice-start.11
  40.4 5.0 %slice-start.12 = ((s8[8486912]{0:T(1024)(128)(4,1)}), s8[4194304]{0:T(1024)(128)(4,1)S(1)}, s32[]{:S(2)}) async-start(s8[8486912]{0:T(1024)(128)(4,1)} %bitcast.42), calls=%async_computation.18 | async-start | bytes 8388608
  40.4 5.4 %slice-start.13 = ((s8[8486912]{0:T(1024)(128)(4,1)}), s8[4194304]{0:T(1024)(128)(4,1)S(1)}, s32[]{:S(2)}) async-start(s8[8486912]{0:T(1024)(128)(4,1)} %bitcast.42), calls=%async_computation.19 | async-start | bytes 8388608
  43.0 2.4 copy-start.7
  43.0 2.8 %slice-start.14 = ((s8[8486912]{0:T(1024)(128)(4,1)}), s8[98304]{0:T(1024)(128)(4,1)S(1)}, s32[]{:S(2)}) async-start(s8[8486912]{0:T(1024)(128)(4,1)} %bitcast.42), calls=%async_computation.20 | async-start | bytes 196608
  43.0 6.0 %slice-start = ((s8[8486912]{0:T(1024)(128)(4,1)}), s8[4194304]{0:T(1024)(128)(4,1)S(1)}, s32[]{:S(2)}) async-start(s8[8486912]{0:T(1024)(128)(4,1)} %bitcast.34), calls=%async_computation.6 | async-start | bytes 8388608
  43.0 6.0 %slice-start.1 = ((s8[8486912]{0:T(1024)(128)(4,1)}), s8[4194304]{0:T(1024)(128)(4,1)S(1)}, s32[]{:S(2)}) async-start(s8[8486912]{0:T(1024)(128)(4,1)} %bitcast.34), calls=%async_computation.7 | async-start | bytes 8388608
  45.8 3.2 %copy-start.9 = (f32[128,1184]{0,1:T(8,128)}, f32[128,1184]{0,1:T(8,128)S(1)}, u32[]{:S(2)}) copy-start(f32[128,1184]{0,1:T(8,128)S(1)} %fusion.11) | copy-start | bytes 1818628
  45.8 3.2 %slice-start.2 = ((s8[8486912]{0:T(1024)(128)(4,1)}), s8[98304]{0:T(1024)(128)(4,1)S(1)}, s32[]{:S(2)}) async-start(s8[8486912]{0:T(1024)(128)(4,1)} %bitcast.34), calls=%async_computation.8 | async-start | bytes 196608
  49.0 2.8 %slice-start.6 = ((s8[8486912]{0:T(1024)(128)(4,1)}), s8[4194304]{0:T(1024)(128)(4,1)S(1)}, s32[]{:S(2)}) async-start(s8[8486912]{0:T(1024)(128)(4,1)} %bitcast.38), calls=%async_computation.12 | async-start | bytes 8388608
  49.1 3.5 %slice-start.7 = ((s8[8486912]{0:T(1024)(128)(4,1)}), s8[4194304]{0:T(1024)(128)(4,1)S(1)}, s32[]{:S(2)}) async-start(s8[8486912]{0:T(1024)(128)(4,1)} %bitcast.38), calls=%async_computation.13 | async-start | bytes 8388608
  50.5 2.1 slice-start.8
  54.0 93.1 %copy-start.12 = (bf16[8,3584]{1,0:T(8,128)(2,1)S(1)}, bf16[8,3584]{1,0:T(8,128)(2,1)}, u32[]{:S(2)}) copy-start(bf16[8,3584]{1,0:T(8,128)(2,1)} %param.9) | copy-start | bytes 172036
  56.1 149.7 %all-gather.4.cloned.1.call-start = ((), (), s32[]{:S(2)}) async-start(), calls=%async_computation.3 | async-start | bytes 2752512 | tf_op jit(solution)/shard_map/all_gather | solution.py:78
  123.9 49.5 %all-to-all-start = ((bf16[16,8,3584]{2,1,0:T(8,128)(2,1)}), bf16[16,8,3584]{2,1,0:T(8,128)(2,1)S(1)}, u32[]{:S(2)}, u32[]{:S(2)}) async-start(bf16[16,8,3584]{2,1,0:T(8,128)(2,1)} %stack.2), calls=%async_computation.1 | async-start | bytes 1835008 | tf_op jit(solution)/shard_map/all_to_all | solution.py:66
  127.6 114.0 %all-gather.6.cloned.1.call-start = ((), (), s32[]{:S(2)}) async-start(), calls=%async_computation.4 | async-start | bytes 2752512 | tf_op jit(solution)/shard_map/all_gather | solution.py:83
  173.2 6.7 %copy-start.3 = (bf16[128,3584]{1,0:T(8,128)(2,1)S(1)}, bf16[128,3584]{1,0:T(8,128)(2,1)}, u32[]{:S(2)}) copy-start(bf16[128,3584]{1,0:T(8,128)(2,1)} %all_gather.28) | copy-start | bytes 2752516
  173.2 78.5 %all-gather.8.cloned.1.call-start = ((), (), s32[]{:S(2)}) async-start(), calls=%async_computation.5 | async-start | bytes 2752512 | tf_op jit(solution)/shard_map/all_gather | solution.py:84
  173.4 6.5 %copy-start.2 = (bf16[16,8,3584]{2,1,0:T(8,128)(2,1)}, bf16[16,8,3584]{2,1,0:T(8,128)(2,1)S(1)}, u32[]{:S(2)}) copy-start(bf16[16,8,3584]{2,1,0:T(8,128)(2,1)S(1)} %all-to-all-done) | copy-start | bytes 2752516
  173.5 12.5 %slice-start.3 = ((s8[8486912]{0:T(1024)(128)(4,1)}), s8[4194304]{0:T(1024)(128)(4,1)S(1)}, s32[]{:S(2)}) async-start(s8[8486912]{0:T(1024)(128)(4,1)} %bitcast.36), calls=%async_computation.9 | async-start | bytes 8388608
  173.5 12.5 %slice-start.4 = ((s8[8486912]{0:T(1024)(128)(4,1)}), s8[4194304]{0:T(1024)(128)(4,1)S(1)}, s32[]{:S(2)}) async-start(s8[8486912]{0:T(1024)(128)(4,1)} %bitcast.36), calls=%async_computation.10 | async-start | bytes 8388608
  179.9 6.0 %slice-start.5 = ((s8[8486912]{0:T(1024)(128)(4,1)}), s8[98304]{0:T(1024)(128)(4,1)S(1)}, s32[]{:S(2)}) async-start(s8[8486912]{0:T(1024)(128)(4,1)} %bitcast.36), calls=%async_computation.11 | async-start | bytes 196608
  179.9 6.0 %copy-start.6 = (f32[128,1184]{0,1:T(8,128)S(1)}, f32[128,1184]{0,1:T(8,128)}, u32[]{:S(2)}) copy-start(f32[128,1184]{0,1:T(8,128)} %copy-done.5) | copy-start | bytes 1818628
  179.9 6.0 %copy-start.8 = (f32[128,1184]{0,1:T(8,128)S(1)}, f32[128,1184]{0,1:T(8,128)}, u32[]{:S(2)}) copy-start(f32[128,1184]{0,1:T(8,128)} %copy-done.7) | copy-start | bytes 1818628
  180.0 6.0 %copy-start.10 = (f32[128,1184]{0,1:T(8,128)S(1)}, f32[128,1184]{0,1:T(8,128)}, u32[]{:S(2)}) copy-start(f32[128,1184]{0,1:T(8,128)} %copy-done.9) | copy-start | bytes 1818628
  180.0 6.0 %copy-start.11 = (f32[128,1184]{0,1:T(8,128)S(1)}, f32[128,1184]{0,1:T(8,128)}, u32[]{:S(2)}) copy-start(f32[128,1184]{0,1:T(8,128)} %get-tuple-element.7) | copy-start | bytes 1818628
  205.8 27.2 %copy-start.4 = (bf16[256,3584]{1,0:T(8,128)(2,1)S(1)}, bf16[256,3584]{1,0:T(8,128)(2,1)}, u32[]{:S(2)}) copy-start(bf16[256,3584]{1,0:T(8,128)(2,1)} %all-gather.4.cloned.1.call-done) | copy-start | bytes 5505028
Sparse Core Ops, SparseCore 0:
  56.2 65.7 reduce-scatter.1
Sparse Core Ops, SparseCore 1:
  58.7 27.2 all-gather.3
  173.3 33.7 all-gather.5
  208.5 36.5 all-gather.7
